TPU v7x, 32 devices: a whole 2x2x4 slice. The times are simulated.
32 devices in a mesh: section: 4 (over x, core), tensor: 4 (over z), dp: 2 (over y).
Axes of the slice: x: 2, y: 2, z: 4, core: 2. Of those that a mesh axis runs over, the one named last changes fastest.
Arguments:
- layer_in: bfloat16 [2, 2, 4, 2, 128, 2560], P(None, None, 'section', 'dp', 'tensor'), may hold values from -6 to 6
- carry_in: bfloat16 [2, 4, 2, 128, 2560], P(None, 'section', 'dp', 'tensor'), may hold values from -6 to 6
- top_grad: bfloat16 [1, 2, 128, 2560], P(None, 'dp', 'tensor'), may hold values from -6 to 6
- w_qkv: bfloat16 [2, 4, 2560, 2560], P(None, 'section', None, 'tensor'), may hold values from -1 to 1
- w_out: bfloat16 [2, 4, 2048, 2560], P(None, 'section', 'tensor'), may hold values from -0.125 to 0.125
- gain: float32 [2, 4, 2560], P(None, 'section'), may hold values from 0.5 to 1.5
Outputs:
- unit_grads: bfloat16 [2, 2, 4, 2, 128, 2560], P(None, None, 'section', 'dp', 'tensor')
- grad_qkv: bfloat16 [2, 4, 2560, 2560], P(None, 'section', 'dp', 'tensor')
- grad_out: bfloat16 [2, 4, 2048, 2560], P(None, 'section', ('tensor', 'dp'))
- grad_gain: float32 [2, 4, 2560], P(None, 'section')
All inputs are finite; a program needn't handle non-finite values.
Results may differ from a plain program's by a relative error of at most 0.022.
The roundings to bfloat16 on the way count: a program that leaves them out, or rounds other values in their place, can miss the bound.
Values may be sent and summed in bfloat16 or wider, within the bound.
A program may use at most 128 MiB of HBM per device.

v0:
```python
import math
import jax
import jax.numpy as jnp
from jax import lax
from jax.sharding import PartitionSpec as P

KV = 4
HD = 64
GROUP = 8
epsilon = 1e-06
rope_base = 1000000.0


def from_behind(value, axis, steps):
    count = lax.axis_size(axis)
    first, last = (max(0, -steps), min(count, count - steps))
    return lax.ppermute(value, axis, [(source, source + steps) for source in range(first, last)])


def rope_tables(length, head_width):
    half_width = head_width // 2
    exponent = jnp.arange(half_width, dtype=jnp.float32) * (2.0 / head_width)
    frequency = rope_base ** (-exponent)
    angle = jnp.arange(length, dtype=jnp.float32)[:, None] * frequency[None, :]
    return (jnp.cos(angle), jnp.sin(angle))


def rotate(values, cosine_table, sine_table, direction):
    half_width = values.shape[-1] // 2
    table_shape = (values.shape[0],) + (1,) * (values.ndim - 2) + (half_width,)
    cosine = cosine_table.reshape(table_shape)
    sine_part = direction * sine_table.reshape(table_shape)
    lower_half = values[..., :half_width]
    upper_half = values[..., half_width:]
    return jnp.concatenate(
        [
            lower_half * cosine - upper_half * sine_part,
            upper_half * cosine + lower_half * sine_part,
        ],
        axis=-1,
    )


def local(layer_in, carry_in, top_grad, w_qkv, w_out, gain):
    ticks = layer_in.shape[0]
    own_rows = layer_in.shape[4]
    length = own_rows * lax.axis_size("tensor")
    kv_local = KV // lax.axis_size("tensor")
    section_index = lax.axis_index("section")
    at_first = section_index == 0
    at_last = section_index == lax.axis_size("section") - 1
    cosine_table, sine_table = rope_tables(length, HD)
    score_scale = 1.0 / math.sqrt(HD)
    causal_mask = jnp.arange(length)[:, None] >= jnp.arange(length)[None, :]
    layer_rows = layer_in[:, :, 0, 0]
    carried = carry_in[:, 0, 0]
    fresh_grads = top_grad[:, 0]
    weight_qkv = w_qkv[:, 0]
    weight_out = w_out[:, 0]
    gain_rows = gain[:, 0]
    contract_rows = (((0,), (0,)), ((), ()))
    contract_cols = (((1,), (1,)), ((), ()))
    qkv_sums = [
        jnp.zeros(weight_qkv.shape[1:], jnp.float32),
        jnp.zeros(weight_qkv.shape[1:], jnp.float32),
    ]
    out_sums = [
        jnp.zeros(weight_out.shape[1:], jnp.float32),
        jnp.zeros(weight_out.shape[1:], jnp.float32),
    ]
    gain_totals = [
        jnp.zeros(gain_rows.shape[1:], jnp.float32),
        jnp.zeros(gain_rows.shape[1:], jnp.float32),
    ]

    def apply_weights(member, stored):
        normed, grad_full, attended, grad_projected = stored
        qkv_sums[member] = qkv_sums[member] + lax.dot_general(
            normed, grad_projected, contract_rows, preferred_element_type=jnp.float32
        )
        out_sums[member] = out_sums[member] + lax.dot_general(
            attended, grad_full, contract_rows, preferred_element_type=jnp.float32
        )

    inputs = [carried[0], carried[1]]
    per_tick = []
    for position in range(ticks):
        outcome = [None, None]
        pending_members = []
        pending_saved = []
        for member in (1, 0):
            layer_part = layer_rows[position, member]
            grad_output = inputs[member]
            inputs_float = layer_part.astype(jnp.float32)
            inverse = lax.rsqrt(
                jnp.mean(inputs_float * inputs_float, axis=-1, keepdims=True) + epsilon
            )
            unit_rows = inputs_float * inverse
            normed_own = (unit_rows * gain_rows[member]).astype(jnp.bfloat16)
            input_normed = lax.all_gather(normed_own, "tensor", axis=0, tiled=True)
            input_grad_full = lax.all_gather(grad_output, "tensor", axis=0, tiled=True)
            projected = jnp.dot(
                input_normed, weight_qkv[member], preferred_element_type=jnp.float32
            )
            projected = projected.reshape(length, kv_local, GROUP + 2, HD)
            query_rot = rotate(projected[:, :, :GROUP], cosine_table, sine_table, 1.0).astype(
                jnp.bfloat16
            )
            key_rot = rotate(projected[:, :, GROUP], cosine_table, sine_table, 1.0).astype(
                jnp.bfloat16
            )
            value_rows = projected[:, :, GROUP + 1].astype(jnp.bfloat16)
            scores = (
                jnp.einsum("tkgd,ukd->kgtu", query_rot, key_rot, preferred_element_type=jnp.float32)
                * score_scale
            )
            scores = jnp.where(causal_mask, scores, -1e30)
            exponentials = jnp.exp(scores - jnp.max(scores, axis=-1, keepdims=True))
            softmax_rows = exponentials / jnp.sum(exponentials, axis=-1, keepdims=True)
            softmax_low = softmax_rows.astype(jnp.bfloat16)
            input_attended = jnp.einsum(
                "kgtu,ukd->tkgd", softmax_low, value_rows, preferred_element_type=jnp.float32
            )
            input_attended = input_attended.astype(jnp.bfloat16).reshape(
                length, kv_local * GROUP * HD
            )
            grad_attended = lax.dot_general(
                input_grad_full,
                weight_out[member],
                contract_cols,
                preferred_element_type=jnp.float32,
            ).astype(jnp.bfloat16)
            grad_heads = grad_attended.reshape(length, kv_local, GROUP, HD)
            grad_softmax = jnp.einsum(
                "tkgd,ukd->kgtu", grad_heads, value_rows, preferred_element_type=jnp.float32
            )
            row_total = jnp.sum(softmax_rows * grad_softmax, axis=-1, keepdims=True)
            grad_scores = (softmax_rows * (grad_softmax - row_total) * score_scale).astype(
                jnp.bfloat16
            )
            grad_value = jnp.einsum(
                "kgtu,tkgd->ukd", softmax_low, grad_heads, preferred_element_type=jnp.float32
            )
            grad_query = rotate(
                jnp.einsum(
                    "kgtu,ukd->tkgd", grad_scores, key_rot, preferred_element_type=jnp.float32
                ),
                cosine_table,
                sine_table,
                -1.0,
            )
            grad_key = rotate(
                jnp.einsum(
                    "kgtu,tkgd->ukd", grad_scores, query_rot, preferred_element_type=jnp.float32
                ),
                cosine_table,
                sine_table,
                -1.0,
            )
            input_grad_projected = jnp.concatenate(
                [grad_query, grad_key[:, :, None], grad_value[:, :, None]], axis=2
            )
            input_grad_projected = input_grad_projected.reshape(
                length, kv_local * (GROUP + 2) * HD
            ).astype(jnp.bfloat16)
            grad_normed = lax.psum_scatter(
                lax.dot_general(
                    input_grad_projected,
                    weight_qkv[member],
                    contract_cols,
                    preferred_element_type=jnp.float32,
                ).astype(jnp.bfloat16),
                "tensor",
                scatter_dimension=0,
                tiled=True,
            ).astype(jnp.float32)
            grad_unit = grad_normed * gain_rows[member]
            grad_rows = inverse * (
                grad_unit - unit_rows * jnp.mean(grad_unit * unit_rows, axis=-1, keepdims=True)
            )
            grad_input = (grad_output.astype(jnp.float32) + grad_rows).astype(jnp.bfloat16)
            grad_scale = jnp.sum(grad_normed * unit_rows, axis=0)
            grad_input, stored, grad_scale = (
                grad_input,
                (input_normed, input_grad_full, input_attended, input_grad_projected),
                grad_scale,
            )
            outcome[member] = grad_input
            gain_totals[member] = gain_totals[member] + grad_scale
            pending_members.append(member)
            pending_saved.append(stored)
        if position + 1 < ticks:
            upward = from_behind(outcome[1], "section", 1)
            downward = from_behind(outcome[0], "section", -1)
            pending_saved, upward, downward = lax.optimization_barrier(
                (pending_saved, upward, downward)
            )
            inputs = [
                jnp.where(at_last, outcome[1], downward),
                jnp.where(at_first, fresh_grads[position], upward),
            ]
        for member, stored in zip(pending_members, pending_saved):
            apply_weights(member, stored)
        per_tick.append(jnp.stack(outcome))
    grad_qkv_all, grad_out_all = (
        lax.psum_scatter(
            jnp.stack(qkv_sums).astype(jnp.bfloat16), "dp", scatter_dimension=1, tiled=True
        ).astype(jnp.float32),
        lax.psum_scatter(
            jnp.stack(out_sums).astype(jnp.bfloat16), "dp", scatter_dimension=1, tiled=True
        ).astype(jnp.float32),
    )
    gain_total = lax.psum(jnp.stack(gain_totals), ("tensor", "dp"))
    unit_grads = jnp.stack(per_tick)[:, :, None, None]
    return (
        unit_grads,
        grad_qkv_all.astype(jnp.bfloat16)[:, None],
        grad_out_all.astype(jnp.bfloat16)[:, None],
        gain_total[:, None],
    )


def solution(mesh):
    in_specs = (
        P(None, None, "section", "dp", "tensor", None),
        P(None, "section", "dp", "tensor", None),
        P(None, "dp", "tensor", None),
        P(None, "section", None, "tensor"),
        P(None, "section", "tensor", None),
        P(None, "section", None),
    )
    out_specs = (
        P(None, None, "section", "dp", "tensor", None),
        P(None, "section", "dp", "tensor"),
        P(None, "section", ("tensor", "dp"), None),
        P(None, "section", None),
    )
    return jax.shard_map(local, mesh=mesh, in_specs=in_specs, out_specs=out_specs, check_vma=False)
```

profile of v0, /device:TPU:0, one launch (start us, length us, event | category | flops | bytes accessed | tf_op | source)
XLA Modules:
  0.0 479.4 jit_solution(15156333436391977317)
XLA Ops:
  7.3 1.2 fusion.91
  10.1 1.7 fusion.181
  11.8 19.7 %all-gather = bf16[1,1,1,128,2560]{4,3,2,1,0:T(8,128)(2,1)S(1)} all-gather(bf16[1,1,1,32,2560]{4,3,2,1,0:T(8,128)(2,1)S(1)} %get-tuple-element.68), channel_id=2, replica_groups=mesh['section'=4,'tensor'=4,'dp'=2] {'tensor'}, dimensions={3}, use_global_device_ids=true | all-gather | bytes 819200 | tf_op jit(solution)/shard_map/all_gather | solution.py:101
  32.3 2.7 fusion.32
  35.4 17.5 %all_gather.24 = bf16[128,2560]{1,0:T(8,128)(2,1)} all-gather(bf16[32,2560]{1,0:T(8,128)(2,1)S(1)} %get-tuple-element.58), channel_id=1, replica_groups=mesh['section'=4,'tensor'=4,'dp'=2] {'tensor'}, dimensions={0}, use_global_device_ids=true | all-gather | bytes 819200 | tf_op jit(solution)/shard_map/all_gather | solution.py:100
  52.9 16.7 %all_gather.26 = bf16[128,2560]{1,0:T(8,128)(2,1)} all-gather(bf16[32,2560]{1,0:T(8,128)(2,1)S(1)} %get-tuple-element.59), channel_id=1, replica_groups=mesh['section'=4,'tensor'=4,'dp'=2] {'tensor'}, dimensions={0}, use_global_device_ids=true | all-gather | bytes 819200 | tf_op jit(solution)/shard_map/all_gather | solution.py:100
  69.6 6.2 %slice_bitcast_fusion.1 = (bf16[640,2560]{0,1:T(8,128)(2,1)}, bf16[640,2560]{0,1:T(8,128)(2,1)}) fusion(bf16[2,1,2560,640]{3,2,1,0:T(8,128)(2,1)} %param.9), kind=kLoop, calls=%fused_computation.30 | loop fusion | bytes 13107200 | tf_op jit(solution)/shard_map/dot_general | solution.py:102
  75.9 4.0 copy.39
  79.9 2.1 convolution_bitcast_fusion.7
  82.7 5.7 %copy.44 = bf16[640,2560]{1,0:T(8,128)(2,1)} copy(bf16[640,2560]{0,1:T(8,128)(2,1)} %get-tuple-element.51) | data formatting | bytes 6553600 | tf_op jit(solution)/shard_map/dot_general | solution.py:102
  88.4 3.2 convolution_bitcast_fusion.6
  95.4 15.2 %all-gather.1 = bf16[1,1,1,128,2560]{4,3,2,1,0:T(8,128)(2,1)S(1)} all-gather(bf16[1,1,1,32,2560]{4,3,2,1,0:T(8,128)(2,1)S(1)} %copy-done.33), channel_id=3, replica_groups=mesh['section'=4,'tensor'=4,'dp'=2] {'tensor'}, dimensions={3}, use_global_device_ids=true | all-gather | bytes 819200 | tf_op jit(solution)/shard_map/all_gather | solution.py:101
  110.6 0.9 copy-done.13
  111.5 3.4 fusion.38
  114.8 1.7 copy.45
  116.5 1.2 fusion.183
  117.9 1.2 convolution_bitcast_fusion.16
  119.2 1.0 multiply_reduce_fusion.2
  123.0 4.0 convolution_convert_fusion.2
  127.1 1.3 convolution_bitcast_fusion.18
  129.2 4.0 convolution_convert_fusion.3
  133.2 2.0 convolution_convert_fusion.6
  135.2 1.9 convolution_convert_fusion.7
  137.2 13.4 %reduce-scatter.9.cloned.1.call-done = bf16[32,2560]{1,0:T(8,128)(2,1)} async-done(((bf16[128,2560]{1,0:T(8,128)(2,1)}), bf16[32,2560]{1,0:T(8,128)(2,1)}) %reduce-scatter.9.cloned.1.call-update) | async-done | bytes 163856 | tf_op jit(solution)/shard_map/reduce_scatter | solution.py:166
  150.5 24.1 %reduce-scatter.7.cloned.1.call-done = bf16[32,2560]{1,0:T(8,128)(2,1)} async-done(((bf16[128,2560]{1,0:T(8,128)(2,1)}), bf16[32,2560]{1,0:T(8,128)(2,1)}) %reduce-scatter.7.cloned.1.call-update) | async-done | bytes 163856 | tf_op jit(solution)/shard_map/reduce_scatter | solution.py:166
  174.7 2.3 fusion.90
  177.1 1.7 fusion.87
  178.8 16.5 %all_gather.30 = bf16[128,2560]{1,0:T(8,128)(2,1)S(1)} all-gather(bf16[32,2560]{1,0:T(8,128)(2,1)S(1)} %get-tuple-element.54), channel_id=1, replica_groups=mesh['section'=4,'tensor'=4,'dp'=2] {'tensor'}, dimensions={0}, use_global_device_ids=true | all-gather | bytes 819200 | tf_op jit(solution)/shard_map/all_gather | solution.py:100
  195.3 1.0 convolution_bitcast_fusion.4
  196.4 15.8 %all_gather.28 = bf16[128,2560]{1,0:T(8,128)(2,1)S(1)} all-gather(bf16[32,2560]{1,0:T(8,128)(2,1)S(1)} %get-tuple-element.55), channel_id=1, replica_groups=mesh['section'=4,'tensor'=4,'dp'=2] {'tensor'}, dimensions={0}, use_global_device_ids=true | all-gather | bytes 819200 | tf_op jit(solution)/shard_map/all_gather | solution.py:100
  212.2 1.0 convolution_bitcast_fusion.5
  213.4 1.4 collective-permute-start.1
  214.8 3.0 collective-permute-start
  218.4 0.9 convolution_convert_fusion.5
  221.0 17.3 %all_gather.29 = bf16[128,2560]{1,0:T(8,128)(2,1)S(1)} all-gather(bf16[32,2560]{1,0:T(8,128)(2,1)S(1)} %broadcast_select_fusion), channel_id=1, replica_groups=mesh['section'=4,'tensor'=4,'dp'=2] {'tensor'}, dimensions={0}, use_global_device_ids=true | all-gather | bytes 819200 | tf_op jit(solution)/shard_map/all_gather | solution.py:101
  238.3 0.9 copy-done.15
  239.3 1.0 fusion.35
  240.4 1.0 multiply_reduce_fusion.1
  242.4 0.9 convolution_bitcast_fusion.9
  244.0 16.7 %all_gather.31 = bf16[128,2560]{1,0:T(8,128)(2,1)S(1)} all-gather(bf16[32,2560]{1,0:T(8,128)(2,1)S(1)} %bitcast_select_fusion), channel_id=1, replica_groups=mesh['section'=4,'tensor'=4,'dp'=2] {'tensor'}, dimensions={0}, use_global_device_ids=true | all-gather | bytes 819200 | tf_op jit(solution)/shard_map/all_gather | solution.py:101
  261.5 3.5 fusion.41
  265.0 1.7 copy.55
  266.8 1.3 convolution_bitcast_fusion.12
  268.1 1.3 multiply_reduce_fusion
  272.2 2.0 convolution_convert_fusion
  274.3 1.0 convolution_convert_fusion.4
  276.0 1.2 convolution_bitcast_fusion.14
  277.3 4.0 convolution_convert_fusion.1
  281.2 3.2 fusion.189
  284.5 3.4 fusion.3
  289.0 0.8 fusion.2
  289.9 2.7 pad_maximum_fusion.1
  293.7 1.0 fusion.186
  294.8 1.0 fusion
  295.9 1.0 fusion.187
  297.0 1.0 fusion.1
  298.0 3.4 pad_maximum_fusion
  302.5 19.2 %reduce-scatter.11.cloned.1.call-done = bf16[32,2560]{1,0:T(8,128)(2,1)} async-done(((bf16[128,2560]{1,0:T(8,128)(2,1)}), bf16[32,2560]{1,0:T(8,128)(2,1)}) %reduce-scatter.11.cloned.1.call-update) | async-done | bytes 163856 | tf_op jit(solution)/shard_map/reduce_scatter | solution.py:166
  321.7 1.4 fusion.98
  323.2 36.0 %psum.7 = f32[2,1,2560]{2,1,0:T(1,128)} all-reduce(f32[2,1,2560]{2,1,0:T(1,128)S(1)} %broadcast_in_dim.33), channel_id=1, replica_groups=mesh['section'=4,'tensor'=4,'dp'=2] {'tensor','dp'}, use_global_device_ids=true, to_apply=%region_30.31 | all-reduce | flops 5120 | bytes 40960 | tf_op jit(solution)/shard_map/psum | solution.py:213
  359.2 1.2 fusion.116
  360.5 0.9 maximum_bitcast_fusion
  361.4 28.5 %reduce-scatter.17.cloned.1.call-done = bf16[2,256,2560]{2,1,0:T(8,128)(2,1)} async-done(((bf16[2,512,2560]{2,1,0:T(8,128)(2,1)}), bf16[2,256,2560]{2,1,0:T(8,128)(2,1)}) %reduce-scatter.17.cloned.1.call-update) | async-done | bytes 2621456 | tf_op jit(solution)/shard_map/reduce_scatter | solution.py:209
  389.9 82.6 %reduce-scatter.15.cloned.1.call-done = bf16[2,1280,640]{2,1,0:T(8,128)(2,1)} async-done(((bf16[2,2560,640]{2,1,0:T(8,128)(2,1)}), bf16[2,1280,640]{2,1,0:T(8,128)(2,1)}) %reduce-scatter.15.cloned.1.call-update) | async-done | bytes 3276816 | tf_op jit(solution)/shard_map/reduce_scatter | solution.py:206
  (287 shorter events, 22.8 us)
Async XLA Ops:
  7.2 28.0 %copy-start.1 = (bf16[2,2,1,1,32,2560]{5,4,3,2,1,0:T(8,128)(2,1)S(1)}, bf16[2,2,1,1,32,2560]{5,4,3,2,1,0:T(8,128)(2,1)}, u32[]{:S(2)}) copy-start(bf16[2,2,1,1,32,2560]{5,4,3,2,1,0:T(8,128)(2,1)} %param.6) | copy-start | bytes 1966084
  7.2 143.4 %reduce-scatter.9.cloned.1.call-start = ((), (), s32[]{:S(2)}) async-start(), calls=%async_computation.7 | async-start | bytes 819200 | tf_op jit(solution)/shard_map/reduce_scatter | solution.py:166
  7.2 84.4 %copy-start.88 = (f32[32]{0:T(128)}, f32[32]{0:T(128)S(1)}, u32[]{:S(2)}) copy-start(f32[32]{0:T(128)S(1)} %negate_power_fusion) | copy-start | bytes 388
  7.3 85.9 %copy-start.49 = (pred[128,128]{0,1:T(8,128)(4,1)}, pred[128,128]{0,1:T(8,128)(4,1)S(1)}, u32[]{:S(2)}) copy-start(pred[128,128]{0,1:T(8,128)(4,1)S(1)} %iota_compare_fusion) | copy-start | bytes 49156
  9.3 26.1 %copy-start.42 = (f32[2560]{0:T(1024)}, f32[2560]{0:T(1024)S(1)}, u32[]{:S(2)}) copy-start(f32[2560]{0:T(1024)S(1)} %get-tuple-element.49) | copy-start | bytes 30724
  10.1 82.3 %copy-start.45 = (f32[128,32]{0,1:T(8,128)}, f32[128,32]{0,1:T(8,128)S(1)}, u32[]{:S(2)}) copy-start(f32[128,32]{0,1:T(8,128)S(1)} %get-tuple-element.112) | copy-start | bytes 49156
  10.1 82.3 %copy-start.59 = (f32[128,32]{0,1:T(8,128)}, f32[128,32]{0,1:T(8,128)S(1)}, u32[]{:S(2)}) copy-start(f32[128,32]{0,1:T(8,128)S(1)} %get-tuple-element.111) | copy-start | bytes 49156
  35.1 58.4 %copy-start.63 = (bf16[128,512]{0,1:T(8,128)(2,1)}, bf16[128,512]{0,1:T(8,128)(2,1)S(1)}, u32[]{:S(2)}) copy-start(bf16[128,512]{0,1:T(8,128)(2,1)S(1)} %copy.40) | copy-start | bytes 393220
  35.2 40.7 %copy-start.92 = (f32[32]{0:T(128)}, f32[32]{0:T(128)S(1)}, u32[]{:S(2)}) copy-start(f32[32]{0:T(128)S(1)} %get-tuple-element.129) | copy-start | bytes 388
  35.2 40.7 %copy-start.94 = (f32[32]{0:T(128)}, f32[32]{0:T(128)S(1)}, u32[]{:S(2)}) copy-start(f32[32]{0:T(128)S(1)} %get-tuple-element.130) | copy-start | bytes 388
  88.4 4.0 copy-start.26
  91.6 3.8 copy-start.27
  116.5 3.8 copy-start.40
  116.5 3.9 copy-start.41
  122.3 4.8 copy-start.80
  122.3 4.8 copy-start.81
  123.0 5.5 %copy-start.54 = (bf16[128,1,8,32]{0,3,2,1:T(8,128)(2,1)S(1)}, bf16[128,1,8,32]{0,3,2,1:T(8,128)(2,1)}, u32[]{:S(2)}) copy-start(bf16[128,1,8,32]{0,3,2,1:T(8,128)(2,1)} %get-tuple-element.74) | copy-start | bytes 196612
  123.0 5.5 %copy-start.55 = (bf16[128,1,8,32]{0,3,2,1:T(8,128)(2,1)S(1)}, bf16[128,1,8,32]{0,3,2,1:T(8,128)(2,1)}, u32[]{:S(2)}) copy-start(bf16[128,1,8,32]{0,3,2,1:T(8,128)(2,1)} %get-tuple-element.75) | copy-start | bytes 196612
  127.0 47.6 %reduce-scatter.7.cloned.1.call-start = ((), (), s32[]{:S(2)}) async-start(), calls=%async_computation.6 | async-start | bytes 819200 | tf_op jit(solution)/shard_map/reduce_scatter | solution.py:166
  128.5 4.8 copy-start.83
  129.2 6.0 %copy-start.77 = (f32[8,128]{1,0:T(8,128)S(1)}, f32[8,128]{1,0:T(8,128)}, u32[]{:S(2)}) copy-start(f32[8,128]{1,0:T(8,128)} %copy-done.76) | copy-start | bytes 12292
  129.2 6.0 %copy-start.86 = (f32[8,128]{1,0:T(8,128)S(1)}, f32[8,128]{1,0:T(8,128)}, u32[]{:S(2)}) copy-start(f32[8,128]{1,0:T(8,128)} %copy-done.85) | copy-start | bytes 12292
  133.1 41.5 %copy-start.43 = (f32[2560]{0:T(1024)S(1)}, f32[2560]{0:T(1024)}, u32[]{:S(2)}) copy-start(f32[2560]{0:T(1024)} %copy-done.42) | copy-start | bytes 30724
  133.2 41.5 %copy-start.93 = (f32[32]{0:T(128)S(1)}, f32[32]{0:T(128)}, u32[]{:S(2)}) copy-start(f32[32]{0:T(128)} %copy-done.92) | copy-start | bytes 388
  133.2 41.5 %copy-start.95 = (f32[32]{0:T(128)S(1)}, f32[32]{0:T(128)}, u32[]{:S(2)}) copy-start(f32[32]{0:T(128)} %copy-done.94) | copy-start | bytes 388
  133.2 169.3 %reduce-scatter.13.cloned.1.call-start = ((), (), s32[]{:S(2)}) async-start(), calls=%async_computation.9 | async-start | bytes 819200 | tf_op jit(solution)/shard_map/reduce_scatter | solution.py:166
  174.7 20.7 %copy-start = (bf16[640,2560]{1,0:T(8,128)(2,1)S(1)}, bf16[640,2560]{1,0:T(8,128)(2,1)}, u32[]{:S(2)}) copy-start(bf16[640,2560]{1,0:T(8,128)(2,1)} %copy.44) | copy-start | bytes 9830404
  177.0 19.3 %copy-start.96 = (f32[32]{0:T(128)}, f32[32]{0:T(128)S(1)}, u32[]{:S(2)}) copy-start(f32[32]{0:T(128)S(1)} %add_rsqrt_fusion) | copy-start | bytes 388
  177.0 19.3 %copy-start.98 = (f32[32]{0:T(128)}, f32[32]{0:T(128)S(1)}, u32[]{:S(2)}) copy-start(f32[32]{0:T(128)S(1)} %add_rsqrt_fusion.1) | copy-start | bytes 388
  178.8 34.6 %copy-start.31 = (bf16[32,2560]{1,0:T(8,128)(2,1)}, bf16[32,2560]{1,0:T(8,128)(2,1)S(1)}, u32[]{:S(2)}) copy-start(bf16[32,2560]{1,0:T(8,128)(2,1)S(1)} %get-tuple-element.52) | copy-start | bytes 491524
  178.8 41.5 %copy-start.19 = (bf16[32,2560]{1,0:T(8,128)(2,1)}, bf16[32,2560]{1,0:T(8,128)(2,1)S(1)}, u32[]{:S(2)}) copy-start(bf16[32,2560]{1,0:T(8,128)(2,1)S(1)} %get-tuple-element.53) | copy-start | bytes 491524
  195.3 17.9 %copy-start.3 = (bf16[128,2560]{1,0:T(8,128)(2,1)}, bf16[128,2560]{1,0:T(8,128)(2,1)S(1)}, u32[]{:S(2)}) copy-start(bf16[128,2560]{1,0:T(8,128)(2,1)S(1)} %all_gather.30) | copy-start | bytes 1966084
  195.3 43.9 %slice-start.2 = ((s8[5242880]{0:T(1024)(128)(4,1)}), s8[1048576]{0:T(1024)(128)(4,1)S(1)}, s32[]{:S(2)}) async-start(s8[5242880]{0:T(1024)(128)(4,1)} %bitcast.493), calls=%async_computation.14 | async-start | bytes 2097152
  196.4 17.0 %copy-start.28 = (f32[128,1,10,64]{0,3,2,1:T(8,128)}, f32[128,1,10,64]{0,3,2,1:T(8,128)S(1)}, u32[]{:S(2)}) copy-start(f32[128,1,10,64]{0,3,2,1:T(8,128)S(1)} %convolution_bitcast_fusion.4) | copy-start | bytes 983044
  196.4 16.9 %copy-start.47 = (f32[128,32]{0,1:T(8,128)S(1)}, f32[128,32]{0,1:T(8,128)}, u32[]{:S(2)}) copy-start(f32[128,32]{0,1:T(8,128)} %copy-done.45) | copy-start | bytes 49156
  196.4 16.9 %copy-start.60 = (f32[128,32]{0,1:T(8,128)S(1)}, f32[128,32]{0,1:T(8,128)}, u32[]{:S(2)}) copy-start(f32[128,32]{0,1:T(8,128)} %copy-done.59) | copy-start | bytes 49156
  196.4 21.4 %copy-start.90 = (f32[32]{0:T(128)S(1)}, f32[32]{0:T(128)}, u32[]{:S(2)}) copy-start(f32[32]{0:T(128)} %copy-done.88) | copy-start | bytes 388
  196.4 21.6 %copy-start.50 = (pred[128,128]{0,1:T(8,128)(4,1)S(1)}, pred[128,128]{0,1:T(8,128)(4,1)}, u32[]{:S(2)}) copy-start(pred[128,128]{0,1:T(8,128)(4,1)} %copy-done.49) | copy-start | bytes 49156
  212.2 6.1 %copy-start.5 = (bf16[128,2560]{1,0:T(8,128)(2,1)}, bf16[128,2560]{1,0:T(8,128)(2,1)S(1)}, u32[]{:S(2)}) copy-start(bf16[128,2560]{1,0:T(8,128)(2,1)S(1)} %all_gather.28) | copy-start | bytes 1966084
  212.2 27.1 %slice-start.3 = ((s8[5242880]{0:T(1024)(128)(4,1)}), s8[4194304]{0:T(1024)(128)(4,1)S(1)}, s32[]{:S(2)}) async-start(s8[5242880]{0:T(1024)(128)(4,1)} %bitcast.493), calls=%async_computation.15 | async-start | bytes 8388608
  213.2 7.1 %copy-start.29 = (f32[128,1,10,64]{0,3,2,1:T(8,128)}, f32[128,1,10,64]{0,3,2,1:T(8,128)S(1)}, u32[]{:S(2)}) copy-start(f32[128,1,10,64]{0,3,2,1:T(8,128)S(1)} %convolution_bitcast_fusion.5) | copy-start | bytes 983044
  213.4 6.9 %collective-permute-start.1 = (bf16[32,2560]{1,0:T(8,128)(2,1)S(1)}, bf16[32,2560]{1,0:T(8,128)(2,1)S(1)}, u32[]{:S(2)}, u32[]{:S(2)}) collective-permute-start(bf16[32,2560]{1,0:T(8,128)(2,1)S(1)} %get-tuple-element.52), channel_id=1, source_target_pairs={{8,0},{16,8},{24,16},{9,1},{17,9},{25,17},{10,2},{18,10},{26,18},{... | collective-permute-start | bytes 491528 | tf_op jit(solution)/shard_map/ppermute | solution.py:17
  214.8 5.5 %collective-permute-start = (bf16[32,2560]{1,0:T(8,128)(2,1)S(1)}, bf16[32,2560]{1,0:T(8,128)(2,1)S(1)}, u32[]{:S(2)}, u32[]{:S(2)}) collective-permute-start(bf16[32,2560]{1,0:T(8,128)(2,1)S(1)} %get-tuple-element.53), channel_id=1, source_target_pairs={{0,8},{8,16},{16,24},{1,9},{9,17},{17,25},{2,10},{10,18},{18,26},{... | collective-permute-start | bytes 491528 | tf_op jit(solution)/shard_map/ppermute | solution.py:17
  218.0 20.3 %copy-start.68 = (bf16[128,32]{0,1:T(8,128)(2,1)}, bf16[128,32]{0,1:T(8,128)(2,1)S(1)}, u32[]{:S(2)}) copy-start(bf16[128,32]{0,1:T(8,128)(2,1)S(1)} %get-tuple-element.104) | copy-start | bytes 24580
  218.0 20.3 %copy-start.70 = (bf16[128,32]{0,1:T(8,128)(2,1)}, bf16[128,32]{0,1:T(8,128)(2,1)S(1)}, u32[]{:S(2)}) copy-start(bf16[128,32]{0,1:T(8,128)(2,1)S(1)} %get-tuple-element.105) | copy-start | bytes 24580
  218.4 23.0 %copy-start.84 = (f32[8,128]{1,0:T(8,128)}, f32[8,128]{1,0:T(8,128)S(1)}, u32[]{:S(2)}) copy-start(f32[8,128]{1,0:T(8,128)S(1)} %fusion.53) | copy-start | bytes 12292
  219.6 18.8 %copy-start.78 = (f32[8,128]{1,0:T(8,128)}, f32[8,128]{1,0:T(8,128)S(1)}, u32[]{:S(2)}) copy-start(f32[8,128]{1,0:T(8,128)S(1)} %get-tuple-element.125) | copy-start | bytes 12292
  261.5 10.7 %slice-start = ((s8[6553600]{0:T(1024)(128)(4,1)}), s8[2359296]{0:T(1024)(128)(4,1)S(1)}, s32[]{:S(2)}) async-start(s8[6553600]{0:T(1024)(128)(4,1)} %bitcast.467), calls=%async_computation.12 | async-start | bytes 4718592
  266.7 4.0 copy-start.30
  266.8 4.0 copy-start.48
  266.8 4.0 copy-start.58
  266.8 5.4 %slice-start.1 = ((s8[6553600]{0:T(1024)(128)(4,1)}), s8[4194304]{0:T(1024)(128)(4,1)S(1)}, s32[]{:S(2)}) async-start(s8[6553600]{0:T(1024)(128)(4,1)} %bitcast.467), calls=%async_computation.13 | async-start | bytes 8388608
  274.2 47.5 %reduce-scatter.11.cloned.1.call-start = ((), (), s32[]{:S(2)}) async-start(), calls=%async_computation.8 | async-start | bytes 819200 | tf_op jit(solution)/shard_map/reduce_scatter | solution.py:166
  276.0 5.2 %copy-start.18 = (bf16[128,2560]{1,0:T(8,128)(2,1)S(1)}, bf16[128,2560]{1,0:T(8,128)(2,1)}, u32[]{:S(2)}) copy-start(bf16[128,2560]{1,0:T(8,128)(2,1)} %copy-done.17) | copy-start | bytes 1966084
  284.4 105.5 %reduce-scatter.17.cloned.1.call-start = ((), (), s32[]{:S(2)}) async-start(), calls=%async_computation.11 | async-start | bytes 7864320 | tf_op jit(solution)/shard_map/reduce_scatter | solution.py:209
  292.6 179.9 %reduce-scatter.15.cloned.1.call-start = ((), (), s32[]{:S(2)}) async-start(), calls=%async_computation.10 | async-start | bytes 9830400 | tf_op jit(solution)/shard_map/reduce_scatter | solution.py:206
  301.4 20.3 %copy-start.2 = (bf16[2,2,1,1,32,2560]{5,4,3,2,1,0:T(8,128)(2,1)S(1)}, bf16[2,2,1,1,32,2560]{5,4,3,2,1,0:T(8,128)(2,1)}, u32[]{:S(2)}) copy-start(bf16[2,2,1,1,32,2560]{5,4,3,2,1,0:T(8,128)(2,1)} %param.6) | copy-start | bytes 1966084
  301.4 20.3 %copy-start.44 = (f32[2560]{0:T(1024)S(1)}, f32[2560]{0:T(1024)}, u32[]{:S(2)}) copy-start(f32[2560]{0:T(1024)} %copy-done.42) | copy-start | bytes 30724
  301.4 20.3 %copy-start.97 = (f32[32]{0:T(128)S(1)}, f32[32]{0:T(128)}, u32[]{:S(2)}) copy-start(f32[32]{0:T(128)} %copy-done.96) | copy-start | bytes 388
  301.4 20.3 %copy-start.99 = (f32[32]{0:T(128)S(1)}, f32[32]{0:T(128)}, u32[]{:S(2)}) copy-start(f32[32]{0:T(128)} %copy-done.98) | copy-start | bytes 388
  301.4 21.6 %copy-start.75 = (f32[2560]{0:T(1024)S(1)}, f32[2560]{0:T(1024)}, u32[]{:S(2)}) copy-start(f32[2560]{0:T(1024)} %get-tuple-element.43) | copy-start | bytes 30724
  301.4 21.7 %copy-start.74 = (f32[2560]{0:T(1024)S(1)}, f32[2560]{0:T(1024)}, u32[]{:S(2)}) copy-start(f32[2560]{0:T(1024)} %get-tuple-element.34) | copy-start | bytes 30724
  301.5 57.7 %copy-start.22 = (bf16[32,2560]{1,0:T(8,128)(2,1)S(1)}, bf16[32,2560]{1,0:T(8,128)(2,1)}, u32[]{:S(2)}) copy-start(bf16[32,2560]{1,0:T(8,128)(2,1)} %copy-done.21) | copy-start | bytes 491524
  301.5 57.7 %copy-start.24 = (bf16[32,2560]{1,0:T(8,128)(2,1)S(1)}, bf16[32,2560]{1,0:T(8,128)(2,1)}, u32[]{:S(2)}) copy-start(bf16[32,2560]{1,0:T(8,128)(2,1)} %copy-done.23) | copy-start | bytes 491524
  (48 other events, 99.7 us)
Sparse Core Ops, SparseCore 0:
  127.1 23.3 reduce-scatter.8
  153.4 21.2 reduce-scatter.6
  274.4 23.2 reduce-scatter.12
  300.4 21.2 reduce-scatter.10
  324.4 65.4 reduce-scatter.16
  392.6 79.8 reduce-scatter.14
where the time goes:
time: 481 us; the launch traced here: 479 us
  blocking collectives  171 us (36%)
  waiting for transfers between devices  168 us (35%)
  matrix products  64 us (13%)
  local copies, waits for them, and re-layouts  32.3 us (7%)
  other arithmetic  23 us (5%)
  between operations  15.6 us (3%)
  starting transfers between devices  4.93 us (1%)
    reduce_scatter x1, waiting for transfers between devices, local(): lax.psum_scatter(jnp.stack(qkv_sums).astype(jnp.bfloat16), 'dp', scatter_...  82.6 us
    all_gather x4, blocking collectives, local(): input_grad_full = lax.all_gather(grad_output, 'tensor', axis=0, tiled=True)  68.9 us
    all_gather x4, blocking collectives, local(): input_normed = lax.all_gather(normed_own, 'tensor', axis=0, tiled=True)  66.6 us
    reduce_scatter x4, waiting for transfers between devices, local(): lax.psum_scatter(lax.dot_general(input_grad_projected, weight_qkv[member]...  56.8 us
    psum x1, blocking collectives, local(): gain_total = lax.psum(jnp.stack(gain_totals), ('tensor', 'dp'))  36 us
    reduce_scatter x1, waiting for transfers between devices, local(): lax.psum_scatter(jnp.stack(out_sums).astype(jnp.bfloat16), 'dp', scatter_...  28.5 us
    dot_general x3, local copies, waits for them, and re-layouts, local(): jnp.dot(input_normed, weight_qkv[member], preferred_element_type=jnp.floa...  15.9 us
    dot_general x4, matrix products, local(): lax.dot_general(input_grad_projected, weight_qkv[member], contract_cols,...  14 us
  transfers between devices with their start and end apart: 8, of which 5 were waited for; matrix products, arithmetic and copies ran while one was open for 8% of the time, Pallas kernels for 0%

commit v1 on v0

--- a/solution.py
+++ b/solution.py
@@ -98,7 +98,14 @@
             unit_rows = inputs_float * inverse
             normed_own = (unit_rows * gain_rows[member]).astype(jnp.bfloat16)
             input_normed = lax.all_gather(normed_own, "tensor", axis=0, tiled=True)
-            input_grad_full = lax.all_gather(grad_output, "tensor", axis=0, tiled=True)
+            size = lax.axis_size("tensor")
+            hops = [(i, (i + 1) % size) for i in range(size)]
+            shards = [grad_output]
+            for hop in range(1, size):
+                shards = [lax.ppermute(shards[0], "tensor", hops), *shards]
+            whole = jnp.concatenate(shards, axis=0)
+            shift = (lax.axis_index("tensor") + 1) * shards[-1].shape[0]
+            input_grad_full = jnp.roll(whole, shift, axis=0)
             projected = jnp.dot(
                 input_normed, weight_qkv[member], preferred_element_type=jnp.float32
             )

time: 481 us -> 463 us (0.963)
  blocking collectives: 171 us -> 104 us
  waiting for transfers between devices: 168 us -> 200 us
  other arithmetic: 23 us -> 31.8 us
  starting transfers between devices: 4.93 us -> 12.5 us
    all_gather x4 -> x0, blocking collectives: 68.9 us -> none  [local(): input_grad_full = lax.all_gather(grad_output, 'tensor', axis=0, tiled=True)]
    ppermute x0 -> x12, waiting for transfers between devices: none -> 35.4 us  [local(): shards = [lax.ppermute(shards[0], 'tensor', hops), *shards]]
    concatenate x0 -> x3, other arithmetic: none -> 8.42 us  [local(): input_grad_full = jnp.roll(whole, shift, axis=0)]
    ppermute x0 -> x12, starting transfers between devices: none -> 7.49 us  [local(): shards = [lax.ppermute(shards[0], 'tensor', hops), *shards]]
    unnamed x208 -> x238, local copies, waits for them, and re-layouts: 10.3 us -> 9.07 us
  transfers between devices with their start and end apart: 8 -> 20, of which waited for: 5 -> 15; matrix products, arithmetic and copies ran while one was open for 8% -> 16% of each run, Pallas kernels for 0% -> 0%
where the time goes in v1:
time: 463 us; the launch traced here: 462 us
  waiting for transfers between devices  200 us (43%)
  blocking collectives  104 us (22%)
  matrix products  65.6 us (14%)
  local copies, waits for them, and re-layouts  31.8 us (7%)
  other arithmetic  31.8 us (7%)
  between operations  15.8 us (3%)
  starting transfers between devices  12.5 us (3%)
    reduce_scatter x1, waiting for transfers between devices, local(): lax.psum_scatter(jnp.stack(qkv_sums).astype(jnp.bfloat16), 'dp', scatter_...  82.6 us
    all_gather x4, blocking collectives, local(): input_normed = lax.all_gather(normed_own, 'tensor', axis=0, tiled=True)  68.1 us
    reduce_scatter x4, waiting for transfers between devices, local(): lax.psum_scatter(lax.dot_general(input_grad_projected, weight_qkv[member]...  52.9 us
    psum x1, blocking collectives, local(): gain_total = lax.psum(jnp.stack(gain_totals), ('tensor', 'dp'))  36 us
    ppermute x12, waiting for transfers between devices, local(): shards = [lax.ppermute(shards[0], 'tensor', hops), *shards]  35.4 us
    reduce_scatter x1, waiting for transfers between devices, local(): lax.psum_scatter(jnp.stack(out_sums).astype(jnp.bfloat16), 'dp', scatter_...  28.5 us
    dot_general x3, local copies, waits for them, and re-layouts, local(): jnp.dot(input_normed, weight_qkv[member], preferred_element_type=jnp.floa...  15.9 us
    dot_general x4, matrix products, local(): lax.dot_general(input_grad_projected, weight_qkv[member], contract_cols,...  14.1 us
  transfers between devices with their start and end apart: 20, of which 15 were waited for; matrix products, arithmetic and copies ran while one was open for 16% of the time, Pallas kernels for 0%

profile of v1, /device:TPU:0, one launch (start us, length us, event | category | flops | bytes accessed | tf_op | source)
XLA Modules:
  0.0 461.8 jit_solution(2611309221550420057)
XLA Ops:
  7.2 1.7 slice_bitcast_fusion.7
  9.0 3.1 collective-permute-start
  12.0 1.6 collective-permute-start.3
  13.6 1.2 fusion.119
  16.6 18.0 %all_gather.12 = bf16[128,2560]{1,0:T(8,128)(2,1)} all-gather(bf16[32,2560]{1,0:T(8,128)(2,1)S(1)} %get-tuple-element.59), channel_id=1, replica_groups=mesh['section'=4,'tensor'=4,'dp'=2] {'tensor'}, dimensions={0}, use_global_device_ids=true | all-gather | bytes 819200 | tf_op jit(solution)/shard_map/all_gather | solution.py:100
  34.5 17.7 %all_gather.13 = bf16[128,2560]{1,0:T(8,128)(2,1)} all-gather(bf16[32,2560]{1,0:T(8,128)(2,1)S(1)} %get-tuple-element.60), channel_id=1, replica_groups=mesh['section'=4,'tensor'=4,'dp'=2] {'tensor'}, dimensions={0}, use_global_device_ids=true | all-gather | bytes 819200 | tf_op jit(solution)/shard_map/all_gather | solution.py:100
  52.2 6.2 %slice_bitcast_fusion.1 = (bf16[640,2560]{0,1:T(8,128)(2,1)}, bf16[640,2560]{0,1:T(8,128)(2,1)}) fusion(bf16[2,1,2560,640]{3,2,1,0:T(8,128)(2,1)} %param.11), kind=kLoop, calls=%fused_computation.30 | loop fusion | bytes 13107200 | tf_op jit(solution)/shard_map/dot_general | solution.py:109
  58.4 4.0 copy.39
  62.5 2.1 convolution_bitcast_fusion.7
  65.3 5.7 %copy.44 = bf16[640,2560]{1,0:T(8,128)(2,1)} copy(bf16[640,2560]{0,1:T(8,128)(2,1)} %get-tuple-element.52) | data formatting | bytes 6553600 | tf_op jit(solution)/shard_map/dot_general | solution.py:109
  71.0 3.2 convolution_bitcast_fusion.6
  75.6 1.1 fusion.208
  77.3 5.5 %collective-permute-done.1 = bf16[32,2560]{1,0:T(8,128)(2,1)} collective-permute-done((bf16[32,2560]{1,0:T(8,128)(2,1)}, bf16[32,2560]{1,0:T(8,128)(2,1)}, u32[]{:S(2)}, u32[]{:S(2)}) %collective-permute-start.1) | collective-permute-done | bytes 163872 | tf_op jit(solution)/shard_map/ppermute | solution.py:105
  83.0 1.7 fusion.79
  84.7 1.6 collective-permute-done.4
  86.3 3.8 collective-permute-done.2
  90.1 2.3 fusion.68
  93.4 2.7 fusion.32
  96.8 1.4 multiply_reduce_fusion.3
  99.5 2.4 fusion.61
  102.8 3.4 fusion.38
  106.2 1.7 copy.45
  107.9 1.4 convolution_bitcast_fusion.16
  109.3 1.1 multiply_reduce_fusion.2
  113.5 4.0 convolution_convert_fusion.2
  118.3 1.3 convolution_bitcast_fusion.18
  120.3 4.0 convolution_convert_fusion.3
  124.6 2.0 convolution_convert_fusion.6
  126.6 1.6 convolution_convert_fusion.7
  128.2 10.4 %reduce-scatter.9.cloned.1.call-done = bf16[32,2560]{1,0:T(8,128)(2,1)} async-done(((bf16[128,2560]{1,0:T(8,128)(2,1)}), bf16[32,2560]{1,0:T(8,128)(2,1)}) %reduce-scatter.9.cloned.1.call-update) | async-done | bytes 163856 | tf_op jit(solution)/shard_map/reduce_scatter | solution.py:173
  138.7 24.2 %reduce-scatter.7.cloned.1.call-done = bf16[32,2560]{1,0:T(8,128)(2,1)} async-done(((bf16[128,2560]{1,0:T(8,128)(2,1)}), bf16[32,2560]{1,0:T(8,128)(2,1)}) %reduce-scatter.7.cloned.1.call-update) | async-done | bytes 163856 | tf_op jit(solution)/shard_map/reduce_scatter | solution.py:173
  162.9 2.3 fusion.118
  165.2 1.7 fusion.115
  167.0 16.6 %all_gather.15 = bf16[128,2560]{1,0:T(8,128)(2,1)S(1)} all-gather(bf16[32,2560]{1,0:T(8,128)(2,1)S(1)} %get-tuple-element.55), channel_id=1, replica_groups=mesh['section'=4,'tensor'=4,'dp'=2] {'tensor'}, dimensions={0}, use_global_device_ids=true | all-gather | bytes 819200 | tf_op jit(solution)/shard_map/all_gather | solution.py:100
  184.7 15.8 %all_gather.14 = bf16[128,2560]{1,0:T(8,128)(2,1)S(1)} all-gather(bf16[32,2560]{1,0:T(8,128)(2,1)S(1)} %get-tuple-element.56), channel_id=1, replica_groups=mesh['section'=4,'tensor'=4,'dp'=2] {'tensor'}, dimensions={0}, use_global_device_ids=true | all-gather | bytes 819200 | tf_op jit(solution)/shard_map/all_gather | solution.py:100
  201.7 1.3 collective-permute-start.7
  203.0 3.0 collective-permute-start.6
  207.2 1.3 collective-permute-start.8
  208.9 5.7 %collective-permute-done.11 = bf16[32,2560]{1,0:T(8,128)(2,1)S(1)} collective-permute-done((bf16[32,2560]{1,0:T(8,128)(2,1)S(1)}, bf16[32,2560]{1,0:T(8,128)(2,1)S(1)}, u32[]{:S(2)}, u32[]{:S(2)}) %collective-permute-start.11) | collective-permute-done | bytes 163872 | tf_op jit(solution)/shard_map/ppermute | solution.py:105
  214.6 3.5 collective-permute-done.8
  219.0 2.7 collective-permute-done.12
  221.7 5.3 %collective-permute-done.9 = bf16[32,2560]{1,0:T(8,128)(2,1)S(1)} collective-permute-done((bf16[32,2560]{1,0:T(8,128)(2,1)S(1)}, bf16[32,2560]{1,0:T(8,128)(2,1)S(1)}, u32[]{:S(2)}, u32[]{:S(2)}) %collective-permute-start.9) | collective-permute-done | bytes 163872 | tf_op jit(solution)/shard_map/ppermute | solution.py:105
  227.9 1.5 collective-permute-done.13
  229.5 5.8 %collective-permute-done.10 = bf16[32,2560]{1,0:T(8,128)(2,1)S(1)} collective-permute-done((bf16[32,2560]{1,0:T(8,128)(2,1)S(1)}, bf16[32,2560]{1,0:T(8,128)(2,1)S(1)}, u32[]{:S(2)}, u32[]{:S(2)}) %collective-permute-start.10) | collective-permute-done | bytes 163872 | tf_op jit(solution)/shard_map/ppermute | solution.py:105
  235.3 3.7 fusion.47
  239.8 2.7 fusion.35
  245.6 3.5 fusion.41
  249.1 1.7 copy.55
  250.8 1.3 convolution_bitcast_fusion.12
  252.1 1.1 multiply_reduce_fusion
  256.3 2.1 convolution_convert_fusion
  260.3 4.0 convolution_convert_fusion.1
  264.4 3.2 fusion.214
  267.9 3.3 fusion.3
  273.2 2.8 pad_maximum_fusion.1
  278.2 1.0 fusion
  279.2 1.0 fusion.212
  281.4 3.4 pad_maximum_fusion
  285.8 18.3 %reduce-scatter.11.cloned.1.call-done = bf16[32,2560]{1,0:T(8,128)(2,1)} async-done(((bf16[128,2560]{1,0:T(8,128)(2,1)}), bf16[32,2560]{1,0:T(8,128)(2,1)}) %reduce-scatter.11.cloned.1.call-update) | async-done | bytes 163856 | tf_op jit(solution)/shard_map/reduce_scatter | solution.py:173
  304.1 1.4 fusion.126
  305.6 36.0 %psum.7 = f32[2,1,2560]{2,1,0:T(1,128)} all-reduce(f32[2,1,2560]{2,1,0:T(1,128)S(1)} %broadcast_in_dim.33), channel_id=1, replica_groups=mesh['section'=4,'tensor'=4,'dp'=2] {'tensor','dp'}, use_global_device_ids=true, to_apply=%region_30.32 | all-reduce | flops 5120 | bytes 40960 | tf_op jit(solution)/shard_map/psum | solution.py:220
  341.6 1.2 fusion.144
  343.8 28.5 %reduce-scatter.17.cloned.1.call-done = bf16[2,256,2560]{2,1,0:T(8,128)(2,1)} async-done(((bf16[2,512,2560]{2,1,0:T(8,128)(2,1)}), bf16[2,256,2560]{2,1,0:T(8,128)(2,1)}) %reduce-scatter.17.cloned.1.call-update) | async-done | bytes 2621456 | tf_op jit(solution)/shard_map/reduce_scatter | solution.py:216
  372.3 82.6 %reduce-scatter.15.cloned.1.call-done = bf16[2,1280,640]{2,1,0:T(8,128)(2,1)} async-done(((bf16[2,2560,640]{2,1,0:T(8,128)(2,1)}), bf16[2,1280,640]{2,1,0:T(8,128)(2,1)}) %reduce-scatter.15.cloned.1.call-update) | async-done | bytes 3276816 | tf_op jit(solution)/shard_map/reduce_scatter | solution.py:213
  (340 shorter events, 34.7 us)
Async XLA Ops:
  7.2 9.2 %copy-start.1 = (bf16[2,2,1,1,32,2560]{5,4,3,2,1,0:T(8,128)(2,1)S(1)}, bf16[2,2,1,1,32,2560]{5,4,3,2,1,0:T(8,128)(2,1)}, u32[]{:S(2)}) copy-start(bf16[2,2,1,1,32,2560]{5,4,3,2,1,0:T(8,128)(2,1)} %param.8) | copy-start | bytes 1966084
  7.2 131.5 %reduce-scatter.9.cloned.1.call-start = ((), (), s32[]{:S(2)}) async-start(), calls=%async_computation.7 | async-start | bytes 819200 | tf_op jit(solution)/shard_map/reduce_scatter | solution.py:173
  9.0 43.2 %copy-start.35 = (bf16[32,2560]{1,0:T(8,128)(2,1)}, bf16[32,2560]{1,0:T(8,128)(2,1)S(1)}, u32[]{:S(2)}) copy-start(bf16[32,2560]{1,0:T(8,128)(2,1)S(1)} %get-tuple-element.70) | copy-start | bytes 491524
  9.0 65.8 %collective-permute-start = (bf16[32,2560]{1,0:T(8,128)(2,1)}, bf16[32,2560]{1,0:T(8,128)(2,1)}, u32[]{:S(2)}, u32[]{:S(2)}) collective-permute-start(bf16[32,2560]{1,0:T(8,128)(2,1)} %get-tuple-element.69), channel_id=1, source_target_pairs={{0,2},{2,4},{4,6},{6,0},{1,3},{3,5},{5,7},{7,1},{8,10},{10,12},{12... | collective-permute-start | bytes 491528 | tf_op jit(solution)/shard_map/ppermute | solution.py:105
  12.0 64.7 %collective-permute-start.3 = (bf16[32,2560]{1,0:T(8,128)(2,1)S(1)}, bf16[32,2560]{1,0:T(8,128)(2,1)}, u32[]{:S(2)}, u32[]{:S(2)}) collective-permute-start(bf16[32,2560]{1,0:T(8,128)(2,1)S(1)} %get-tuple-element.70), channel_id=1, source_target_pairs={{0,2},{2,4},{4,6},{6,0},{1,3},{3,5},{5,7},{7,1},{8,10},{10,12},{12... | collective-permute-start | bytes 491528 | tf_op jit(solution)/shard_map/ppermute | solution.py:105
  13.6 60.6 %copy-start.105 = (f32[32]{0:T(128)}, f32[32]{0:T(128)S(1)}, u32[]{:S(2)}) copy-start(f32[32]{0:T(128)S(1)} %negate_power_fusion) | copy-start | bytes 388
  13.6 62.0 %copy-start.56 = (pred[128,128]{0,1:T(8,128)(4,1)}, pred[128,128]{0,1:T(8,128)(4,1)S(1)}, u32[]{:S(2)}) copy-start(pred[128,128]{0,1:T(8,128)(4,1)S(1)} %iota_compare_fusion) | copy-start | bytes 49156
  14.8 43.6 %copy-start.113 = (f32[32]{0:T(128)}, f32[32]{0:T(128)S(1)}, u32[]{:S(2)}) copy-start(f32[32]{0:T(128)S(1)} %add_rsqrt_fusion.3) | copy-start | bytes 388
  14.8 43.6 %copy-start.115 = (f32[32]{0:T(128)}, f32[32]{0:T(128)S(1)}, u32[]{:S(2)}) copy-start(f32[32]{0:T(128)S(1)} %add_rsqrt_fusion.2) | copy-start | bytes 388
  15.6 42.8 %copy-start.49 = (f32[2560]{0:T(1024)}, f32[2560]{0:T(1024)S(1)}, u32[]{:S(2)}) copy-start(f32[2560]{0:T(1024)S(1)} %get-tuple-element.50) | copy-start | bytes 30724
  16.4 58.0 %copy-start.52 = (f32[128,32]{0,1:T(8,128)}, f32[128,32]{0,1:T(8,128)S(1)}, u32[]{:S(2)}) copy-start(f32[128,32]{0,1:T(8,128)S(1)} %get-tuple-element.113) | copy-start | bytes 49156
  74.1 8.8 %copy-start.29 = (f32[128,1,10,64]{0,3,2,1:T(8,128)}, f32[128,1,10,64]{0,3,2,1:T(8,128)S(1)}, u32[]{:S(2)}) copy-start(f32[128,1,10,64]{0,3,2,1:T(8,128)S(1)} %convolution_bitcast_fusion.6) | copy-start | bytes 983044
  74.3 8.6 %copy-start.77 = (bf16[128,32]{0,1:T(8,128)(2,1)}, bf16[128,32]{0,1:T(8,128)(2,1)S(1)}, u32[]{:S(2)}) copy-start(bf16[128,32]{0,1:T(8,128)(2,1)S(1)} %get-tuple-element.109) | copy-start | bytes 24580
  74.3 8.6 %copy-start.79 = (bf16[128,32]{0,1:T(8,128)(2,1)}, bf16[128,32]{0,1:T(8,128)(2,1)S(1)}, u32[]{:S(2)}) copy-start(bf16[128,32]{0,1:T(8,128)(2,1)S(1)} %get-tuple-element.110) | copy-start | bytes 24580
  74.4 8.6 %copy-start.81 = (bf16[128,32]{0,1:T(8,128)(2,1)}, bf16[128,32]{0,1:T(8,128)(2,1)S(1)}, u32[]{:S(2)}) copy-start(bf16[128,32]{0,1:T(8,128)(2,1)S(1)} %get-tuple-element.89) | copy-start | bytes 24580
  74.4 8.6 %copy-start.83 = (bf16[128,32]{0,1:T(8,128)(2,1)}, bf16[128,32]{0,1:T(8,128)(2,1)S(1)}, u32[]{:S(2)}) copy-start(bf16[128,32]{0,1:T(8,128)(2,1)S(1)} %get-tuple-element.90) | copy-start | bytes 24580
  74.5 8.5 %copy-start.43 = (bf16[128,8,32]{0,2,1:T(8,128)(2,1)}, bf16[128,8,32]{0,2,1:T(8,128)(2,1)S(1)}, u32[]{:S(2)}) copy-start(bf16[128,8,32]{0,2,1:T(8,128)(2,1)S(1)} %get-tuple-element.101) | copy-start | bytes 196612
  74.5 8.5 %copy-start.45 = (bf16[128,8,32]{0,2,1:T(8,128)(2,1)}, bf16[128,8,32]{0,2,1:T(8,128)(2,1)S(1)}, u32[]{:S(2)}) copy-start(bf16[128,8,32]{0,2,1:T(8,128)(2,1)S(1)} %get-tuple-element.102) | copy-start | bytes 196612
  74.5 8.5 %copy-start.47 = (bf16[128,8,32]{0,2,1:T(8,128)(2,1)}, bf16[128,8,32]{0,2,1:T(8,128)(2,1)S(1)}, u32[]{:S(2)}) copy-start(bf16[128,8,32]{0,2,1:T(8,128)(2,1)S(1)} %get-tuple-element.66) | copy-start | bytes 196612
  74.8 8.0 %copy-start.9 = (f32[1,8,128,128]{2,3,1,0:T(8,128)}, f32[1,8,128,128]{2,3,1,0:T(8,128)S(1)}, u32[]{:S(2)}) copy-start(f32[1,8,128,128]{2,3,1,0:T(8,128)S(1)} %get-tuple-element.115) | copy-start | bytes 1572868
  74.8 8.0 %collective-permute-start.1 = (bf16[32,2560]{1,0:T(8,128)(2,1)}, bf16[32,2560]{1,0:T(8,128)(2,1)}, u32[]{:S(2)}, u32[]{:S(2)}) collective-permute-start(bf16[32,2560]{1,0:T(8,128)(2,1)} %collective-permute-done), channel_id=1, source_target_pairs={{0,2},{2,4},{4,6},{6,0},{1,3},{3,5},{5,7},{7,1},{8,10},{10,12},{12... | collective-permute-start | bytes 491528 | tf_op jit(solution)/shard_map/ppermute | solution.py:105
  76.7 19.4 %copy-start.91 = (f32[8,128]{1,0:T(8,128)}, f32[8,128]{1,0:T(8,128)S(1)}, u32[]{:S(2)}) copy-start(f32[8,128]{1,0:T(8,128)S(1)} %get-tuple-element.118) | copy-start | bytes 12292
  76.7 9.6 %collective-permute-start.4 = (bf16[32,2560]{1,0:T(8,128)(2,1)}, bf16[32,2560]{1,0:T(8,128)(2,1)}, u32[]{:S(2)}, u32[]{:S(2)}) collective-permute-start(bf16[32,2560]{1,0:T(8,128)(2,1)} %collective-permute-done.3), channel_id=1, source_target_pairs={{0,2},{2,4},{4,6},{6,0},{1,3},{3,5},{5,7},{7,1},{8,10},{10,12},{12... | collective-permute-start | bytes 491528 | tf_op jit(solution)/shard_map/ppermute | solution.py:105
  82.8 7.3 %collective-permute-start.2 = (bf16[32,2560]{1,0:T(8,128)(2,1)}, bf16[32,2560]{1,0:T(8,128)(2,1)S(1)}, u32[]{:S(2)}, u32[]{:S(2)}) collective-permute-start(bf16[32,2560]{1,0:T(8,128)(2,1)} %collective-permute-done.1), channel_id=1, source_target_pairs={{0,2},{2,4},{4,6},{6,0},{1,3},{3,5},{5,7},{7,1},{8,10},{10,12},{12... | collective-permute-start | bytes 491528 | tf_op jit(solution)/shard_map/ppermute | solution.py:105
  83.0 15.4 %copy-start.98 = (f32[8,128]{1,0:T(8,128)}, f32[8,128]{1,0:T(8,128)S(1)}, u32[]{:S(2)}) copy-start(f32[8,128]{1,0:T(8,128)S(1)} %fusion.77) | copy-start | bytes 12292
  86.3 13.2 %collective-permute-start.5 = (bf16[32,2560]{1,0:T(8,128)(2,1)}, bf16[32,2560]{1,0:T(8,128)(2,1)}, u32[]{:S(2)}, u32[]{:S(2)}) collective-permute-start(bf16[32,2560]{1,0:T(8,128)(2,1)} %collective-permute-done.4), channel_id=1, source_target_pairs={{0,2},{2,4},{4,6},{6,0},{1,3},{3,5},{5,7},{7,1},{8,10},{10,12},{12... | collective-permute-start | bytes 491528 | tf_op jit(solution)/shard_map/ppermute | solution.py:105
  117.5 45.4 %reduce-scatter.7.cloned.1.call-start = ((), (), s32[]{:S(2)}) async-start(), calls=%async_computation.6 | async-start | bytes 819200 | tf_op jit(solution)/shard_map/reduce_scatter | solution.py:173
  124.3 161.5 %reduce-scatter.13.cloned.1.call-start = ((), (), s32[]{:S(2)}) async-start(), calls=%async_computation.9 | async-start | bytes 819200 | tf_op jit(solution)/shard_map/reduce_scatter | solution.py:173
  126.6 36.3 %copy-start.50 = (f32[2560]{0:T(1024)S(1)}, f32[2560]{0:T(1024)}, u32[]{:S(2)}) copy-start(f32[2560]{0:T(1024)} %copy-done.49) | copy-start | bytes 30724
  126.6 36.3 %copy-start.114 = (f32[32]{0:T(128)S(1)}, f32[32]{0:T(128)}, u32[]{:S(2)}) copy-start(f32[32]{0:T(128)} %copy-done.113) | copy-start | bytes 388
  126.6 36.3 %copy-start.116 = (f32[32]{0:T(128)S(1)}, f32[32]{0:T(128)}, u32[]{:S(2)}) copy-start(f32[32]{0:T(128)} %copy-done.115) | copy-start | bytes 388
  162.9 20.8 %copy-start = (bf16[640,2560]{1,0:T(8,128)(2,1)S(1)}, bf16[640,2560]{1,0:T(8,128)(2,1)}, u32[]{:S(2)}) copy-start(bf16[640,2560]{1,0:T(8,128)(2,1)} %copy.44) | copy-start | bytes 9830404
  167.0 34.7 %copy-start.33 = (bf16[32,2560]{1,0:T(8,128)(2,1)}, bf16[32,2560]{1,0:T(8,128)(2,1)S(1)}, u32[]{:S(2)}) copy-start(bf16[32,2560]{1,0:T(8,128)(2,1)S(1)} %get-tuple-element.53) | copy-start | bytes 491524
  167.0 40.2 %copy-start.21 = (bf16[32,2560]{1,0:T(8,128)(2,1)}, bf16[32,2560]{1,0:T(8,128)(2,1)S(1)}, u32[]{:S(2)}) copy-start(bf16[32,2560]{1,0:T(8,128)(2,1)S(1)} %get-tuple-element.54) | copy-start | bytes 491524
  184.6 16.9 %copy-start.30 = (f32[128,1,10,64]{0,3,2,1:T(8,128)}, f32[128,1,10,64]{0,3,2,1:T(8,128)S(1)}, u32[]{:S(2)}) copy-start(f32[128,1,10,64]{0,3,2,1:T(8,128)S(1)} %convolution_bitcast_fusion.4) | copy-start | bytes 983044
  200.5 6.5 %copy-start.63 = (bf16[1,1,32,2560]{3,2,1,0:T(8,128)(2,1)S(1)}, bf16[1,1,32,2560]{3,2,1,0:T(8,128)(2,1)}, u32[]{:S(2)}) copy-start(bf16[1,1,32,2560]{3,2,1,0:T(8,128)(2,1)} %param.10) | copy-start | bytes 491524
  201.5 16.6 %copy-start.31 = (f32[128,1,10,64]{0,3,2,1:T(8,128)}, f32[128,1,10,64]{0,3,2,1:T(8,128)S(1)}, u32[]{:S(2)}) copy-start(f32[128,1,10,64]{0,3,2,1:T(8,128)S(1)} %convolution_bitcast_fusion.5) | copy-start | bytes 983044
  201.5 7.0 %copy-start.57 = (pred[128,128]{0,1:T(8,128)(4,1)S(1)}, pred[128,128]{0,1:T(8,128)(4,1)}, u32[]{:S(2)}) copy-start(pred[128,128]{0,1:T(8,128)(4,1)} %copy-done.56) | copy-start | bytes 49156
  201.7 4.5 collective-permute-start.7
  203.0 4.0 collective-permute-start.6
  206.2 20.8 %copy-start.85 = (bf16[128,32]{0,1:T(8,128)(2,1)}, bf16[128,32]{0,1:T(8,128)(2,1)S(1)}, u32[]{:S(2)}) copy-start(bf16[128,32]{0,1:T(8,128)(2,1)S(1)} %get-tuple-element.105) | copy-start | bytes 24580
  206.2 20.8 %copy-start.87 = (bf16[128,32]{0,1:T(8,128)(2,1)}, bf16[128,32]{0,1:T(8,128)(2,1)S(1)}, u32[]{:S(2)}) copy-start(bf16[128,32]{0,1:T(8,128)(2,1)S(1)} %get-tuple-element.106) | copy-start | bytes 24580
  207.1 28.3 %copy-start.23 = (bf16[32,2560]{1,0:T(8,128)(2,1)}, bf16[32,2560]{1,0:T(8,128)(2,1)S(1)}, u32[]{:S(2)}) copy-start(bf16[32,2560]{1,0:T(8,128)(2,1)S(1)} %bitcast_select_fusion) | copy-start | bytes 491524
  207.1 7.5 %collective-permute-start.11 = (bf16[32,2560]{1,0:T(8,128)(2,1)S(1)}, bf16[32,2560]{1,0:T(8,128)(2,1)S(1)}, u32[]{:S(2)}, u32[]{:S(2)}) collective-permute-start(bf16[32,2560]{1,0:T(8,128)(2,1)S(1)} %bitcast_select_fusion), channel_id=1, source_target_pairs={{0,2},{2,4},{4,6},{6,0},{1,3},{3,5},{5,7},{7,1},{8,10},{10,12},{12... | collective-permute-start | bytes 491528 | tf_op jit(solution)/shard_map/ppermute | solution.py:105
  207.2 28.1 %copy-start.25 = (bf16[32,2560]{1,0:T(8,128)(2,1)}, bf16[32,2560]{1,0:T(8,128)(2,1)S(1)}, u32[]{:S(2)}) copy-start(bf16[32,2560]{1,0:T(8,128)(2,1)S(1)} %broadcast_select_fusion) | copy-start | bytes 491524
  207.2 10.9 %collective-permute-start.8 = (bf16[32,2560]{1,0:T(8,128)(2,1)S(1)}, bf16[32,2560]{1,0:T(8,128)(2,1)S(1)}, u32[]{:S(2)}, u32[]{:S(2)}) collective-permute-start(bf16[32,2560]{1,0:T(8,128)(2,1)S(1)} %broadcast_select_fusion), channel_id=1, source_target_pairs={{0,2},{2,4},{4,6},{6,0},{1,3},{3,5},{5,7},{7,1},{8,10},{10,12},{12... | collective-permute-start | bytes 491528 | tf_op jit(solution)/shard_map/ppermute | solution.py:105
  208.9 34.8 %copy-start.100 = (f32[8,128]{1,0:T(8,128)}, f32[8,128]{1,0:T(8,128)S(1)}, u32[]{:S(2)}) copy-start(f32[8,128]{1,0:T(8,128)S(1)} %fusion.81) | copy-start | bytes 12292
  214.6 7.1 %collective-permute-start.12 = (bf16[32,2560]{1,0:T(8,128)(2,1)S(1)}, bf16[32,2560]{1,0:T(8,128)(2,1)S(1)}, u32[]{:S(2)}, u32[]{:S(2)}) collective-permute-start(bf16[32,2560]{1,0:T(8,128)(2,1)S(1)} %collective-permute-done.11), channel_id=1, source_target_pairs={{0,2},{2,4},{4,6},{6,0},{1,3},{3,5},{5,7},{7,1},{8,10},{10,12},{12... | collective-permute-start | bytes 491528 | tf_op jit(solution)/shard_map/ppermute | solution.py:105
  218.1 8.9 %collective-permute-start.9 = (bf16[32,2560]{1,0:T(8,128)(2,1)S(1)}, bf16[32,2560]{1,0:T(8,128)(2,1)S(1)}, u32[]{:S(2)}, u32[]{:S(2)}) collective-permute-start(bf16[32,2560]{1,0:T(8,128)(2,1)S(1)} %collective-permute-done.8), channel_id=1, source_target_pairs={{0,2},{2,4},{4,6},{6,0},{1,3},{3,5},{5,7},{7,1},{8,10},{10,12},{12... | collective-permute-start | bytes 491528 | tf_op jit(solution)/shard_map/ppermute | solution.py:105
  221.7 7.8 %collective-permute-start.13 = (bf16[32,2560]{1,0:T(8,128)(2,1)S(1)}, bf16[32,2560]{1,0:T(8,128)(2,1)S(1)}, u32[]{:S(2)}, u32[]{:S(2)}) collective-permute-start(bf16[32,2560]{1,0:T(8,128)(2,1)S(1)} %collective-permute-done.12), channel_id=1, source_target_pairs={{0,2},{2,4},{4,6},{6,0},{1,3},{3,5},{5,7},{7,1},{8,10},{10,12},{12... | collective-permute-start | bytes 491528 | tf_op jit(solution)/shard_map/ppermute | solution.py:105
  226.9 8.4 %collective-permute-start.10 = (bf16[32,2560]{1,0:T(8,128)(2,1)S(1)}, bf16[32,2560]{1,0:T(8,128)(2,1)S(1)}, u32[]{:S(2)}, u32[]{:S(2)}) collective-permute-start(bf16[32,2560]{1,0:T(8,128)(2,1)S(1)} %collective-permute-done.9), channel_id=1, source_target_pairs={{0,2},{2,4},{4,6},{6,0},{1,3},{3,5},{5,7},{7,1},{8,10},{10,12},{12... | collective-permute-start | bytes 491528 | tf_op jit(solution)/shard_map/ppermute | solution.py:105
  227.2 11.8 %copy-start.94 = (f32[8,128]{1,0:T(8,128)}, f32[8,128]{1,0:T(8,128)S(1)}, u32[]{:S(2)}) copy-start(f32[8,128]{1,0:T(8,128)S(1)} %get-tuple-element.126) | copy-start | bytes 12292
  245.6 10.7 %slice-start = ((s8[6553600]{0:T(1024)(128)(4,1)}), s8[2359296]{0:T(1024)(128)(4,1)S(1)}, s32[]{:S(2)}) async-start(s8[6553600]{0:T(1024)(128)(4,1)} %bitcast.465), calls=%async_computation.12 | async-start | bytes 4718592
  258.4 45.8 %reduce-scatter.11.cloned.1.call-start = ((), (), s32[]{:S(2)}) async-start(), calls=%async_computation.8 | async-start | bytes 819200 | tf_op jit(solution)/shard_map/reduce_scatter | solution.py:173
  267.6 104.7 %reduce-scatter.17.cloned.1.call-start = ((), (), s32[]{:S(2)}) async-start(), calls=%async_computation.11 | async-start | bytes 7864320 | tf_op jit(solution)/shard_map/reduce_scatter | solution.py:216
  276.0 178.9 %reduce-scatter.15.cloned.1.call-start = ((), (), s32[]{:S(2)}) async-start(), calls=%async_computation.10 | async-start | bytes 9830400 | tf_op jit(solution)/shard_map/reduce_scatter | solution.py:213
  284.8 19.3 %copy-start.2 = (bf16[2,2,1,1,32,2560]{5,4,3,2,1,0:T(8,128)(2,1)S(1)}, bf16[2,2,1,1,32,2560]{5,4,3,2,1,0:T(8,128)(2,1)}, u32[]{:S(2)}) copy-start(bf16[2,2,1,1,32,2560]{5,4,3,2,1,0:T(8,128)(2,1)} %param.8) | copy-start | bytes 1966084
  284.8 19.3 %copy-start.51 = (f32[2560]{0:T(1024)S(1)}, f32[2560]{0:T(1024)}, u32[]{:S(2)}) copy-start(f32[2560]{0:T(1024)} %copy-done.49) | copy-start | bytes 30724
  284.8 19.3 %copy-start.110 = (f32[32]{0:T(128)S(1)}, f32[32]{0:T(128)}, u32[]{:S(2)}) copy-start(f32[32]{0:T(128)} %copy-done.109) | copy-start | bytes 388
  284.8 19.3 %copy-start.112 = (f32[32]{0:T(128)S(1)}, f32[32]{0:T(128)}, u32[]{:S(2)}) copy-start(f32[32]{0:T(128)} %copy-done.111) | copy-start | bytes 388
  284.8 20.7 %copy-start.90 = (f32[2560]{0:T(1024)S(1)}, f32[2560]{0:T(1024)}, u32[]{:S(2)}) copy-start(f32[2560]{0:T(1024)} %get-tuple-element.44) | copy-start | bytes 30724
  284.9 20.7 %copy-start.89 = (f32[2560]{0:T(1024)S(1)}, f32[2560]{0:T(1024)}, u32[]{:S(2)}) copy-start(f32[2560]{0:T(1024)} %get-tuple-element.35) | copy-start | bytes 30724
  284.9 56.7 %copy-start.24 = (bf16[32,2560]{1,0:T(8,128)(2,1)S(1)}, bf16[32,2560]{1,0:T(8,128)(2,1)}, u32[]{:S(2)}) copy-start(bf16[32,2560]{1,0:T(8,128)(2,1)} %copy-done.23) | copy-start | bytes 491524
  284.9 56.7 %copy-start.26 = (bf16[32,2560]{1,0:T(8,128)(2,1)S(1)}, bf16[32,2560]{1,0:T(8,128)(2,1)}, u32[]{:S(2)}) copy-start(bf16[32,2560]{1,0:T(8,128)(2,1)} %copy-done.25) | copy-start | bytes 491524
  (75 other events, 125.6 us)
Sparse Core Ops, SparseCore 0:
  117.6 21.0 reduce-scatter.8
  141.5 21.2 reduce-scatter.6
  258.5 22.1 reduce-scatter.12
  282.8 21.2 reduce-scatter.10
  306.8 65.4 reduce-scatter.16
  375.0 79.8 reduce-scatter.14
